TPU v7x, 32 devices: a whole 2x2x4 slice. The times are simulated.
32 devices in a mesh: groups: 2 (over x), row: 8 (over z, y), head: 2 (over core).
Axes of the slice: x: 2, y: 2, z: 4, core: 2. Of those that a mesh axis runs over, the one named last changes fastest.
Arguments:
- hidden: bfloat16 [48, 4096], P('groups'), parts along dimension 0, may hold values from -6 to 6
- norm_gain: float32 [4096], replicated, may hold values from 0.1 to 1.9
- w_query: bfloat16 [8, 256, 4096], P('head', 'row'), may hold values from -0.09375 to 0.09375
- w_key: bfloat16 [8, 256, 4096], P('head', 'row'), may hold values from -0.09375 to 0.09375
- w_value: bfloat16 [8, 512, 4096], P('head', 'row'), may hold values from -0.09375 to 0.09375
- w_outgate: bfloat16 [8, 512, 4096], P('head', 'row'), may hold values from -0.09375 to 0.09375
- w_out: bfloat16 [8, 512, 4096], P('head', 'row'), may hold values from -0.125 to 0.125
- w_gates: bfloat16 [2, 8, 4096], P(None, 'head'), may hold values from -0.09375 to 0.09375
- gate_bias: float32 [2, 8], P(None, 'head'), may hold values from -2 to 4
- headnorm_gain: float32 [8, 512], P('head', 'row'), may hold values from 0.1 to 1.9
- final_gain: float32 [4096], replicated, may hold values from 0.1 to 1.9
- w_vocab: bfloat16 [25152, 4096], P(('row', 'head')), may hold values from -39.0625 to 39.0625
- memory: float32 [48, 8, 256, 512], P('groups', 'head', 'row'), parts along dimension 0, may hold values from -6 to 6
- normalizer: float32 [48, 8, 256], P('groups', 'head', 'row'), parts along dimension 0, may hold values from -6 to 6
- stabilizer: float32 [48, 8], P('groups', 'head'), parts along dimension 0, may hold values from -2 to 2
- targets: int32 [48], P('groups'), parts along dimension 0, may hold values from 0 to 25151
Outputs:
- memory_out: float32 [48, 8, 256, 512], P('groups', 'head', 'row'), parts along dimension 0
- normalizer_out: float32 [48, 8, 256], P('groups', 'head', 'row'), parts along dimension 0
- stabilizer_out: float32 [48, 8], P('groups', 'head'), parts along dimension 0
- hidden_out: bfloat16 [48, 4096], P('groups', ('row', 'head')), parts along dimension 0
- log_prob: float32 [48], P('groups'), parts along dimension 0
There are 2 independent parts, one for each index of `groups`. A program takes and returns all parts, laid end to end along the dimension named above; an argument that names none is the same for every part. Nothing has to cross between parts.
All inputs are finite; a program needn't handle non-finite values.
Results may differ from a plain program's by a relative error of at most 0.0035.
The roundings to bfloat16 on the way count: a program that leaves them out, or rounds other values in their place, can miss the bound.
Values may be sent and summed in bfloat16 or wider, within the bound.
A program may use at most 64 MiB of HBM per device.

v0:
```python
import math
import jax
import jax.numpy as jnp
from jax import lax
from jax.sharding import PartitionSpec as P

QK_DIM = 256
epsilon = 1e-06


def joined_2(value, axis, join):
    pieces = jax.tree.map(lambda part: lax.all_gather(part, axis), value)
    head = jax.tree.map(lambda part: part[0], pieces)
    tail = jax.tree.map(lambda part: part[1:], pieces)
    total, _ = lax.scan(lambda total, share: (join(total, share), None), head, tail)
    return total


def rms_round(stream, gain):
    scale = lax.rsqrt(jnp.mean(stream * stream, axis=-1, keepdims=True) + epsilon)
    return (stream * scale * gain).astype(jnp.bfloat16)


def per_device(
    hidden,
    norm_gain,
    w_query,
    w_key,
    w_value,
    w_outgate,
    w_out,
    w_gates,
    gate_bias,
    headnorm_gain,
    final_gain,
    w_vocab,
    memory,
    normalizer,
    stabilizer,
    targets,
):
    value_rows = w_value.shape[1]
    stream = hidden.astype(jnp.float32)
    normed_in = rms_round(stream, norm_gain)

    def project(weights):
        return jnp.einsum("sd,hjd->shj", normed_in, weights, preferred_element_type=jnp.float32)

    queries = project(w_query) / math.sqrt(QK_DIM)
    key_part = project(w_key)
    value_part = project(w_value).astype(jnp.bfloat16)
    outgate_pre = project(w_outgate)
    gate_pre = (
        jnp.einsum("sd,ghd->gsh", normed_in, w_gates, preferred_element_type=jnp.float32)
        + gate_bias[:, None, :]
    )
    log_forget = jax.nn.log_sigmoid(gate_pre[1])
    stabilizer_out = jnp.maximum(log_forget + stabilizer, gate_pre[0])
    decay_rate = jnp.exp(log_forget + stabilizer - stabilizer_out)
    inflow = jnp.exp(gate_pre[0] - stabilizer_out)
    scaled_key = inflow[:, :, None] * key_part
    memory_out = (
        decay_rate[:, :, None, None] * memory
        + scaled_key[:, :, :, None]
        * lax.all_gather(value_part, "row", axis=2, tiled=True).astype(jnp.float32)[:, :, None, :]
    )
    normalizer_out = decay_rate[:, :, None] * normalizer + scaled_key
    partial_readout = jnp.einsum(
        "shj,shje->she", queries, memory_out, precision=lax.Precision.HIGHEST
    )
    readout = lax.psum(partial_readout, "row")
    average = jnp.mean(readout, axis=-1)
    centered_full = readout - average[:, :, None]
    variance = jnp.mean(centered_full * centered_full, axis=-1)
    centered = lax.dynamic_slice_in_dim(
        centered_full, lax.axis_index("row") * value_rows, value_rows, 2
    )
    normed = centered * lax.rsqrt(variance + epsilon)[:, :, None] * headnorm_gain
    gated_out = (jax.nn.sigmoid(outgate_pre) * normed).astype(jnp.bfloat16)
    partial_terms = jnp.einsum("shj,hjd->sd", gated_out, w_out, preferred_element_type=jnp.float32)
    position = lax.axis_index("row") * lax.axis_size("head") + lax.axis_index("head")
    share_width = hidden.shape[1] // (lax.axis_size("row") * lax.axis_size("head"))
    vocab_here = w_vocab.shape[0]
    projection = lax.psum(partial_terms, ("row", "head"))
    new_full = (stream + projection).astype(jnp.bfloat16)
    final_feat = rms_round(new_full.astype(jnp.float32), final_gain)
    logits = jnp.einsum("sd,vd->sv", final_feat, w_vocab, preferred_element_type=jnp.float32)
    hidden_out = lax.dynamic_slice_in_dim(new_full, position * share_width, share_width, 1)
    local_ids = targets - position * vocab_here
    is_target = jnp.arange(vocab_here, dtype=jnp.int32)[None, :] == local_ids[:, None]
    target_term = jnp.sum(jnp.where(is_target, logits, 0.0), axis=-1)
    local_max = jnp.max(logits, axis=-1)
    local_sum = jnp.sum(jnp.exp(logits - local_max[:, None]), axis=-1)

    def combine(earlier, later):
        highest = jnp.maximum(earlier[0], later[0])
        joined = earlier[1] * jnp.exp(earlier[0] - highest) + later[1] * jnp.exp(later[0] - highest)
        return (highest, joined, earlier[2] + later[2])

    highest, exp_total, picked = joined_2(
        (local_max, local_sum, target_term), ("row", "head"), combine
    )
    log_prob = picked - (highest + jnp.log(exp_total))
    return (memory_out, normalizer_out, stabilizer_out, hidden_out, log_prob)


def solution(mesh):
    in_specs = (
        P("groups", None),
        P(),
        P("head", "row", None),
        P("head", "row", None),
        P("head", "row", None),
        P("head", "row", None),
        P("head", "row", None),
        P(None, "head", None),
        P(None, "head"),
        P("head", "row"),
        P(),
        P(("row", "head"), None),
        P("groups", "head", "row", None),
        P("groups", "head", "row"),
        P("groups", "head"),
        P("groups"),
    )
    out_specs = (
        P("groups", "head", "row", None),
        P("groups", "head", "row"),
        P("groups", "head"),
        P("groups", ("row", "head")),
        P("groups"),
    )
    return jax.shard_map(
        per_device, mesh=mesh, in_specs=in_specs, out_specs=out_specs, check_vma=False
    )
```

profile of v0, /device:TPU:0, one launch (start us, length us, event | category | flops | bytes accessed | tf_op | source)
XLA Modules:
  0.0 280.0 jit_solution(1592682969917463788)
XLA Ops:
  7.2 0.0 copy-start
  7.2 0.0 all-reduce.7.cloned.1.call-start
  7.2 1.2 fusion.17
  8.5 2.7 convolution_convert_fusion
  11.1 0.1 copy.34
  11.3 33.0 %all_gather.21 = bf16[24,4,512]{0,1,2:T(4,128)(2,1)S(1)} all-gather(bf16[24,4,64]{0,1,2:T(4,128)(2,1)S(1)} %copy.34), channel_id=1, replica_groups=mesh['groups'=2,'row'=8,'head'=2] {'row'}, dimensions={2}, use_global_device_ids=true | all-gather | bytes 110592 | tf_op jit(solution)/shard_map/all_gather | solution.py:65
  44.3 0.3 copy.35
  44.6 0.1 copy.36
  44.7 1.2 fusion.13
  45.9 0.7 subtract_exponential_fusion.1
  46.6 0.0 copy-start.5
  46.6 0.1 copy.32
  46.7 2.2 fusion.28
  48.9 2.2 fusion.7
  51.1 3.4 %multiply_add_fusion = f32[24,4,32,512]{3,2,1,0:T(8,128)S(1)} fusion(f32[24,4,32,512]{3,2,1,0:T(8,128)} %param.30, f32[24,4,512]{2,1,0:T(4,128)S(1)} %copy.36, f32[24,4,32]{2,1,0:T(4,128)S(1)} %copy.33, f32[24,4]{1,0:T(8,128)S(1)} %copy.32), kind=kLoop, calls=%fused_computation.10 | loop fusion | flops 4718592 | bytes 12792192 | tf_op jit(solution)/shard_map/add | solution.py:63
  54.5 0.0 copy-start.1
  54.5 2.7 copy-done.1
  57.2 0.0 copy-start.7
  57.2 0.0 copy-start.4
  57.2 3.1 %fusion.26 = f32[24,4,1,512]{3,2,1,0:T(1,128)S(1)} fusion(f32[24,4,32,512]{3,2,1,0:T(8,128)S(1)} %multiply_add_fusion, f32[24,4,32,1]{2,0,1,3:T(8,128)S(1)} %fusion.7), kind=kOutput, calls=%fused_computation.46 | convolution fusion | flops 18874368 | bytes 6500352 | tf_op jit(solution)/shard_map/shj,shje->she/dot_general | solution.py:68
  60.4 0.7 copy.47
  61.1 0.0 all-reduce.7.cloned.1.call-update
  61.1 0.0 all-reduce.9.cloned.1.call-start
  61.2 0.6 copy.38
  61.8 0.6 dynamic-slice
  63.1 70.0 %all-reduce.7.cloned.1.call-done = f32[24,4,512]{2,0,1:T(8,128)} async-done(((f32[24,4,512]{2,0,1:T(8,128)}), f32[24,4,512]{2,0,1:T(8,128)}) %all-reduce.7.cloned.1.call-update) | async-done | bytes 196624 | tf_op jit(solution)/shard_map/psum | solution.py:71
  133.1 1.0 reduce_sum.55
  134.1 1.1 multiply_reduce_fusion
  135.3 3.8 %convolution_bitcast_fusion = f32[24,4096]{1,0:T(8,128)} fusion(bf16[4,64,4096]{2,1,0:T(8,128)(2,1)S(1)} %copy-done, bf16[4,64,4096]{2,1,0:T(8,128)(2,1)} %param.23, f32[24,4,512]{2,0,1:T(8,128)S(1)} %get-tuple-element.86, s32[]{:T(128)S(6)} %select_n.16, f32[4,64]{1,0:T(4,128)S(1)} %copy-done.6, f32[24,4]{0,1:T(4,128)S(1)} %add_rsqrt_fusion, ...), kind=kOutput, calls=%fused_computation.11 | convolution fusion | flops 101099520 | bytes 4854276 | tf_op jit(solution)/shard_map/shj,hjd->sd/dot_general | solution.py:80
  139.0 0.0 all-reduce.9.cloned.1.call-update
  139.1 90.6 %all-reduce.9.cloned.1.call-done = f32[24,4096]{1,0:T(8,128)} async-done(((f32[24,4096]{1,0:T(8,128)}), f32[24,4096]{1,0:T(8,128)}) %all-reduce.9.cloned.1.call-update) | async-done | bytes 393232 | tf_op jit(solution)/shard_map/psum | solution.py:84
  229.6 1.2 fusion.14
  230.8 0.0 copy-done.4
  230.8 8.3 %fusion.50 = (f32[24]{0:T(128)S(1)}, f32[24,1572]{1,0:T(8,128)S(1)}) fusion(bf16[1572,4096]{1,0:T(8,128)(2,1)} %param.29, bf16[24,4096]{1,0:T(8,128)(2,1)S(1)} %get-tuple-element.84, f32[4096]{0:T(1024)S(1)} %copy-done.4, f32[24]{0:T(128)S(1)} %add_rsqrt_fusion.1), kind=kOutput, calls=%fused_computation.74 | convolution fusion | flops 309498688 | bytes 13241920 | tf_op jit(solution)/shard_map/sd,vd->sv/dot_general | solution.py:87
  239.1 0.2 dynamic-update-slice
  239.3 0.2 select_reduce_fusion
  239.6 0.2 dynamic-update-slice.1
  239.8 0.2 dynamic-update-slice.2
  240.0 30.9 %all-reduce.3 = (f32[384]{0:T(512)S(1)}, f32[384]{0:T(512)S(1)}, f32[384]{0:T(512)S(1)}) all-reduce(f32[384]{0:T(512)S(1)} %dynamic-update-slice, f32[384]{0:T(512)S(1)} %dynamic-update-slice.1, f32[384]{0:T(512)S(1)} %dynamic-update-slice.2), channel_id=2, replica_groups=mesh['groups'=2,'row'=8,'head'=2] {'row','head'}, use_global_device_ids=true, to_apply=%add | all-reduce | flops 1152 | bytes 9216
  271.0 0.1 slice.36
  271.0 0.1 slice.37
  271.1 0.1 slice.38
  271.2 0.6 constant_dynamic-slice_fusion.3
  271.8 0.1 reshape.55
  271.9 0.1 reshape.56
  271.9 0.1 reshape.57
  272.0 0.6 while.14
  272.7 0.5 add_subtract_fusion
  (39 shorter events, 0.5 us)
Async XLA Ops:
  7.2 128.1 %copy-start = (bf16[4,64,4096]{2,1,0:T(8,128)(2,1)S(1)}, bf16[4,64,4096]{2,1,0:T(8,128)(2,1)}, u32[]{:S(2)}) copy-start(bf16[4,64,4096]{2,1,0:T(8,128)(2,1)} %param.24) | copy-start | bytes 6291460
  7.2 125.9 %all-reduce.7.cloned.1.call-start = ((), (), s32[]{:S(2)}) async-start(), calls=%async_computation | async-start | bytes 393216 | tf_op jit(solution)/shard_map/psum | solution.py:71
  46.6 7.9 %copy-start.5 = (f32[24,4]{0,1:T(4,128)}, f32[24,4]{0,1:T(4,128)S(1)}, u32[]{:S(2)}) copy-start(f32[24,4]{0,1:T(4,128)S(1)} %get-tuple-element.88) | copy-start | bytes 1156
  54.5 2.7 copy-start.1
  57.2 4.6 %copy-start.8 = (u32[32]{0:T(128)S(1)}, u32[32]{0:T(128)}, u32[]{:S(2)}) copy-start(u32[32]{0:T(128)} %constant.57) | copy-start | bytes 388
  57.2 78.0 %copy-start.2 = (bf16[24,4096]{1,0:T(8,128)(2,1)S(1)}, bf16[24,4096]{1,0:T(8,128)(2,1)}, u32[]{:S(2)}) copy-start(bf16[24,4096]{1,0:T(8,128)(2,1)} %param.18) | copy-start | bytes 589828
  57.2 78.0 %copy-start.3 = (f32[4096]{0:T(1024)S(1)}, f32[4096]{0:T(1024)}, u32[]{:S(2)}) copy-start(f32[4096]{0:T(1024)} %param.19) | copy-start | bytes 49156
  57.2 78.1 %copy-start.6 = (f32[4,64]{1,0:T(4,128)S(1)}, f32[4,64]{1,0:T(4,128)}, u32[]{:S(2)}) copy-start(f32[4,64]{1,0:T(4,128)} %param.27) | copy-start | bytes 3076
  57.2 81.8 %copy-start.7 = (s32[24]{0:T(128)S(1)}, s32[24]{0:T(128)}, u32[]{:S(2)}) copy-start(s32[24]{0:T(128)} %param.33) | copy-start | bytes 292
  57.2 173.6 %copy-start.4 = (f32[4096]{0:T(1024)S(1)}, f32[4096]{0:T(1024)}, u32[]{:S(2)}) copy-start(f32[4096]{0:T(1024)} %param.28) | copy-start | bytes 49156
  61.1 168.5 %all-reduce.9.cloned.1.call-start = ((), (), s32[]{:S(2)}) async-start(), calls=%async_computation.1 | async-start | bytes 786432 | tf_op jit(solution)/shard_map/psum | solution.py:84
Sparse Core Ops, SparseCore 0:
  61.2 71.7 all-reduce.6
  139.2 90.4 all-reduce.8
where the time goes:
time: 281 us; the launch traced here: 280 us
  waiting for transfers between devices  161 us (57%)
  blocking collectives  64 us (23%)
  matrix products  23.4 us (8%)
  between operations  15 us (5%)
  other arithmetic  9.78 us (3%)
  local copies, waits for them, and re-layouts  7.02 us (2%)
    psum x1, waiting for transfers between devices, per_device(): projection = lax.psum(partial_terms, ('row', 'head'))  90.6 us
    psum x1, waiting for transfers between devices, per_device(): readout = lax.psum(partial_readout, 'row')  70 us
    all_gather x1, blocking collectives, per_device(): lax.all_gather(value_part, 'row', axis=2, tiled=True).astype(jnp.float32)  33 us
    unnamed x1, blocking collectives  30.9 us
    dot_general x1, matrix products, per_device(): jnp.einsum('sd,vd->sv', final_feat, w_vocab, preferred_element_type=jnp.f...  8.26 us
    dot_general x3, matrix products, project(): jnp.einsum('sd,hjd->shj', normed_in, weights, preferred_element_type=jnp....  7.03 us
  transfers between devices with their start and end apart: 2, of which 2 were waited for; matrix products, arithmetic and copies ran while one was open for 0% of the time, Pallas kernels for 0%

commit v1 on v0

--- a/solution.py
+++ b/solution.py
@@ -81,7 +81,8 @@
     position = lax.axis_index("row") * lax.axis_size("head") + lax.axis_index("head")
     share_width = hidden.shape[1] // (lax.axis_size("row") * lax.axis_size("head"))
     vocab_here = w_vocab.shape[0]
-    projection = lax.psum(partial_terms, ("row", "head"))
+    partial = lax.psum(partial_terms, "row")
+    projection = lax.psum(partial, "head")
     new_full = (stream + projection).astype(jnp.bfloat16)
     final_feat = rms_round(new_full.astype(jnp.float32), final_gain)
     logits = jnp.einsum("sd,vd->sv", final_feat, w_vocab, preferred_element_type=jnp.float32)

time: 281 us -> 284 us (1.011)
  blocking collectives: 64 us -> 67.4 us
    unnamed x1, blocking collectives: 30.9 us -> 34.4 us
    psum x1 -> x2, waiting for transfers between devices: 90.6 us -> 88.9 us  [the longest x1 71 us: per_device(): partial = lax.psum(partial_terms, 'row')]
  transfers between devices with their start and end apart: 2 -> 3, of which waited for: 2 -> 3; matrix products, arithmetic and copies ran while one was open for 0% -> 0% of each run, Pallas kernels for 0% -> 0%
where the time goes in v1:
time: 284 us; the launch traced here: 283 us
  waiting for transfers between devices  161 us (57%)
  blocking collectives  67.4 us (24%)
  matrix products  23.4 us (8%)
  between operations  14.7 us (5%)
  other arithmetic  9.78 us (3%)
  local copies, waits for them, and re-layouts  7.02 us (2%)
    psum x1, waiting for transfers between devices, per_device(): readout = lax.psum(partial_readout, 'row')  71.9 us
    psum x1, waiting for transfers between devices, per_device(): partial = lax.psum(partial_terms, 'row')  71 us
    unnamed x1, blocking collectives  34.4 us
    all_gather x1, blocking collectives, per_device(): lax.all_gather(value_part, 'row', axis=2, tiled=True).astype(jnp.float32)  33 us
    psum x1, waiting for transfers between devices, per_device(): projection = lax.psum(partial, 'head')  17.9 us
    dot_general x1, matrix products, per_device(): jnp.einsum('sd,vd->sv', final_feat, w_vocab, preferred_element_type=jnp.f...  8.26 us
    dot_general x3, matrix products, project(): jnp.einsum('sd,hjd->shj', normed_in, weights, preferred_element_type=jnp....  7.03 us
  transfers between devices with their start and end apart: 3, of which 3 were waited for; matrix products, arithmetic and copies ran while one was open for 0% of the time, Pallas kernels for 0%

profile of v1, /device:TPU:0, one launch (start us, length us, event | category | flops | bytes accessed | tf_op | source)
XLA Modules:
  0.0 283.4 jit_solution(493557090273110360)
XLA Ops:
  7.2 0.0 copy-start
  7.2 0.0 all-reduce.8.cloned.1.call-start
  7.2 1.2 fusion.17
  8.5 2.7 convolution_convert_fusion
  11.1 0.1 copy.34
  11.3 33.0 %all_gather.21 = bf16[24,4,512]{0,1,2:T(4,128)(2,1)S(1)} all-gather(bf16[24,4,64]{0,1,2:T(4,128)(2,1)S(1)} %copy.34), channel_id=1, replica_groups=mesh['groups'=2,'row'=8,'head'=2] {'row'}, dimensions={2}, use_global_device_ids=true | all-gather | bytes 110592 | tf_op jit(solution)/shard_map/all_gather | solution.py:65
  44.3 0.3 copy.35
  44.6 0.1 copy.36
  44.7 1.2 fusion.13
  45.9 0.7 subtract_exponential_fusion.1
  46.6 0.1 copy.32
  46.7 2.2 fusion.28
  48.9 2.2 fusion.7
  51.1 3.4 %multiply_add_fusion = f32[24,4,32,512]{3,2,1,0:T(8,128)S(1)} fusion(f32[24,4,32,512]{3,2,1,0:T(8,128)} %param.30, f32[24,4,512]{2,1,0:T(4,128)S(1)} %copy.36, f32[24,4,32]{2,1,0:T(4,128)S(1)} %copy.33, f32[24,4]{1,0:T(8,128)S(1)} %copy.32), kind=kLoop, calls=%fused_computation.10 | loop fusion | flops 4718592 | bytes 12792192 | tf_op jit(solution)/shard_map/add | solution.py:63
  54.5 0.0 copy-start.1
  54.5 2.7 copy-done.1
  57.2 0.0 copy-start.4
  57.2 3.1 %fusion.26 = f32[24,4,1,512]{3,2,1,0:T(1,128)S(1)} fusion(f32[24,4,32,512]{3,2,1,0:T(8,128)S(1)} %multiply_add_fusion, f32[24,4,32,1]{2,0,1,3:T(8,128)S(1)} %fusion.7), kind=kOutput, calls=%fused_computation.46 | convolution fusion | flops 18874368 | bytes 6500352 | tf_op jit(solution)/shard_map/shj,shje->she/dot_general | solution.py:68
  60.4 0.7 copy.47
  61.1 0.0 all-reduce.8.cloned.1.call-update
  61.1 0.0 all-reduce.10.cloned.1.call-start
  61.2 71.9 %all-reduce.8.cloned.1.call-done = f32[24,4,512]{2,0,1:T(8,128)} async-done(((f32[24,4,512]{2,0,1:T(8,128)}), f32[24,4,512]{2,0,1:T(8,128)}) %all-reduce.8.cloned.1.call-update) | async-done | bytes 196624 | tf_op jit(solution)/shard_map/psum | solution.py:71
  133.1 1.0 reduce_sum.55
  134.1 1.1 multiply_reduce_fusion
  135.3 3.8 %convolution_bitcast_fusion = f32[24,4096]{1,0:T(8,128)} fusion(bf16[4,64,4096]{2,1,0:T(8,128)(2,1)S(1)} %copy-done, bf16[4,64,4096]{2,1,0:T(8,128)(2,1)} %param.23, f32[24,4,512]{2,0,1:T(8,128)S(1)} %get-tuple-element.86, s32[]{:T(128)S(6)} %select_n.16, f32[4,64]{1,0:T(4,128)S(1)} %copy-done.6, f32[24,4]{0,1:T(4,128)S(1)} %add_rsqrt_fusion, ...), kind=kOutput, calls=%fused_computation.11 | convolution fusion | flops 101099520 | bytes 4854276 | tf_op jit(solution)/shard_map/shj,hjd->sd/dot_general | solution.py:80
  139.0 0.0 all-reduce.10.cloned.1.call-update
  139.0 0.0 all-reduce.12.cloned.1.call-start
  139.1 71.0 %all-reduce.10.cloned.1.call-done = f32[24,4096]{1,0:T(8,128)} async-done(((f32[24,4096]{1,0:T(8,128)}), f32[24,4096]{1,0:T(8,128)}) %all-reduce.10.cloned.1.call-update) | async-done | bytes 393232 | tf_op jit(solution)/shard_map/psum | solution.py:84
  210.0 0.0 all-reduce.12.cloned.1.call-update
  210.1 0.6 copy.38
  210.7 0.6 dynamic-slice
  212.0 17.9 %all-reduce.12.cloned.1.call-done = f32[24,4096]{1,0:T(8,128)} async-done(((f32[24,4096]{1,0:T(8,128)}), f32[24,4096]{1,0:T(8,128)}) %all-reduce.12.cloned.1.call-update) | async-done | bytes 393232 | tf_op jit(solution)/shard_map/psum | solution.py:85
  229.9 1.2 fusion.14
  231.0 8.3 %fusion.50 = (f32[24]{0:T(128)S(1)}, f32[24,1572]{1,0:T(8,128)S(1)}) fusion(bf16[1572,4096]{1,0:T(8,128)(2,1)} %param.29, bf16[24,4096]{1,0:T(8,128)(2,1)S(1)} %get-tuple-element.84, f32[4096]{0:T(1024)S(1)} %copy-done.4, f32[24]{0:T(128)S(1)} %add_rsqrt_fusion.1), kind=kOutput, calls=%fused_computation.74 | convolution fusion | flops 309498688 | bytes 13241920 | tf_op jit(solution)/shard_map/sd,vd->sv/dot_general | solution.py:88
  239.3 0.2 dynamic-update-slice
  239.6 0.2 select_reduce_fusion
  239.8 0.2 dynamic-update-slice.1
  240.0 0.2 dynamic-update-slice.2
  240.2 34.4 %all-reduce.3 = (f32[384]{0:T(512)S(1)}, f32[384]{0:T(512)S(1)}, f32[384]{0:T(512)S(1)}) all-reduce(f32[384]{0:T(512)S(1)} %dynamic-update-slice, f32[384]{0:T(512)S(1)} %dynamic-update-slice.1, f32[384]{0:T(512)S(1)} %dynamic-update-slice.2), channel_id=2, replica_groups=mesh['groups'=2,'row'=8,'head'=2] {'row','head'}, use_global_device_ids=true, to_apply=%add | all-reduce | flops 1152 | bytes 9216
  274.6 0.1 slice.36
  274.7 0.1 slice.37
  274.8 0.1 slice.38
  274.8 0.6 constant_dynamic-slice_fusion.3
  275.4 0.1 reshape.55
  275.5 0.1 reshape.56
  275.6 0.1 reshape.57
  275.7 0.6 while.14
  276.3 0.5 add_subtract_fusion
  (42 shorter events, 0.5 us)
Async XLA Ops:
  7.2 128.1 %copy-start = (bf16[4,64,4096]{2,1,0:T(8,128)(2,1)S(1)}, bf16[4,64,4096]{2,1,0:T(8,128)(2,1)}, u32[]{:S(2)}) copy-start(bf16[4,64,4096]{2,1,0:T(8,128)(2,1)} %param.24) | copy-start | bytes 6291460
  7.2 125.9 %all-reduce.8.cloned.1.call-start = ((), (), s32[]{:S(2)}) async-start(), calls=%async_computation | async-start | bytes 393216 | tf_op jit(solution)/shard_map/psum | solution.py:71
  46.6 7.9 %copy-start.5 = (f32[24,4]{0,1:T(4,128)}, f32[24,4]{0,1:T(4,128)S(1)}, u32[]{:S(2)}) copy-start(f32[24,4]{0,1:T(4,128)S(1)} %get-tuple-element.88) | copy-start | bytes 1156
  54.5 2.7 copy-start.1
  57.2 78.0 %copy-start.2 = (bf16[24,4096]{1,0:T(8,128)(2,1)S(1)}, bf16[24,4096]{1,0:T(8,128)(2,1)}, u32[]{:S(2)}) copy-start(bf16[24,4096]{1,0:T(8,128)(2,1)} %param.18) | copy-start | bytes 589828
  57.2 78.0 %copy-start.3 = (f32[4096]{0:T(1024)S(1)}, f32[4096]{0:T(1024)}, u32[]{:S(2)}) copy-start(f32[4096]{0:T(1024)} %param.19) | copy-start | bytes 49156
  57.2 78.1 %copy-start.6 = (f32[4,64]{1,0:T(4,128)S(1)}, f32[4,64]{1,0:T(4,128)}, u32[]{:S(2)}) copy-start(f32[4,64]{1,0:T(4,128)} %param.27) | copy-start | bytes 3076
  57.2 153.5 %copy-start.8 = (u32[32]{0:T(128)S(1)}, u32[32]{0:T(128)}, u32[]{:S(2)}) copy-start(u32[32]{0:T(128)} %constant.57) | copy-start | bytes 388
  57.2 154.7 %copy-start.7 = (s32[24]{0:T(128)S(1)}, s32[24]{0:T(128)}, u32[]{:S(2)}) copy-start(s32[24]{0:T(128)} %param.33) | copy-start | bytes 292
  57.2 173.8 %copy-start.4 = (f32[4096]{0:T(1024)S(1)}, f32[4096]{0:T(1024)}, u32[]{:S(2)}) copy-start(f32[4096]{0:T(1024)} %param.28) | copy-start | bytes 49156
  61.1 148.9 %all-reduce.10.cloned.1.call-start = ((), (), s32[]{:S(2)}) async-start(), calls=%async_computation.1 | async-start | bytes 786432 | tf_op jit(solution)/shard_map/psum | solution.py:84
  139.0 90.8 %all-reduce.12.cloned.1.call-start = ((), (), s32[]{:S(2)}) async-start(), calls=%async_computation.2 | async-start | bytes 786432 | tf_op jit(solution)/shard_map/psum | solution.py:85
Sparse Core Ops, SparseCore 0:
  61.2 71.7 all-reduce.7
  139.2 70.8 all-reduce.9
  212.4 17.4 all-reduce.11
